TPU v7x, 16 devices: a whole 2x2x2 slice. The times are simulated.
16 devices in a mesh: dp: 4 (over z, y), stage: 4 (over x, core).
Axes of the slice: x: 2, y: 2, z: 2, core: 2. Of those that a mesh axis runs over, the one named last changes fastest.
Arguments:
- tokens_in: bfloat16 [128, 256, 512], P('dp'), parts along dimension 0
- targets: bfloat16 [128, 256, 512], P('dp'), parts along dimension 0
- w_in: bfloat16 [8, 512, 2048], P('stage')
- w_out: bfloat16 [8, 2048, 512], P('stage')
- norm_gains: float32 [8, 512], P('stage')
Outputs:
- output 1: float32 [32, 512, 2048], P(('dp', 'stage')), parts along dimension 0
- output 2: float32 [32, 2048, 512], P(('dp', 'stage')), parts along dimension 0
- output 3: float32 [32, 512], P(('dp', 'stage')), parts along dimension 0
- output 4: float32 [4], P('dp'), parts along dimension 0
There are 4 independent parts. A program takes and returns all parts, laid end to end along the dimension named above; an argument that names none is the same for every part.
All inputs are finite; a program needn't handle non-finite values.
Results may differ from a plain program's by a relative error of at most 0.00280117.
Values are sent between devices in bfloat16 or wider.
A program may use at most 1 GiB of HBM per device.

v0:
```python
import jax
import jax.numpy as jnp
from jax import lax
from jax.sharding import PartitionSpec as P

EPSILON = 1e-6


def norm_scale(x_f32, gain_vec):
    inv_rms = lax.rsqrt(jnp.mean(x_f32 * x_f32, axis=-1, keepdims=True) + EPSILON)
    return x_f32 * inv_rms * gain_vec


def layer_forward(x_act, first_w, second_w, gain_vec):
    x_f32 = x_act.astype(jnp.float32)
    normed = norm_scale(x_f32, gain_vec).astype(jnp.bfloat16)
    pre_act = jnp.dot(normed, first_w, preferred_element_type=jnp.float32)
    hidden = jax.nn.gelu(pre_act).astype(jnp.bfloat16)
    out_f32 = jnp.dot(hidden, second_w, preferred_element_type=jnp.float32)
    return (x_f32 + out_f32).astype(jnp.bfloat16)


def layer_backward(x_act, grad_h, first_w, second_w, gain_vec):
    x_f32 = x_act.astype(jnp.float32)
    normed_f32, norm_vjp = jax.vjp(norm_scale, x_f32, gain_vec)
    normed = normed_f32.astype(jnp.bfloat16)
    pre_act = jnp.dot(normed, first_w, preferred_element_type=jnp.float32)
    hidden_f32, gelu_vjp = jax.vjp(jax.nn.gelu, pre_act)
    hidden = hidden_f32.astype(jnp.bfloat16)
    grad_second = jnp.einsum('tf,td->fd', hidden, grad_h, preferred_element_type=jnp.float32)
    grad_hidden = jnp.einsum('td,fd->tf', grad_h, second_w, preferred_element_type=jnp.float32)
    grad_pre = gelu_vjp(grad_hidden)[0].astype(jnp.bfloat16)
    grad_first = jnp.einsum('td,tf->df', normed, grad_pre, preferred_element_type=jnp.float32)
    grad_normed = jnp.einsum('tf,df->td', grad_pre, first_w, preferred_element_type=jnp.float32)
    grad_x_norm, grad_gain = norm_vjp(grad_normed)
    grad_x = (grad_h.astype(jnp.float32) + grad_x_norm).astype(jnp.bfloat16)
    return grad_x, grad_first, grad_second, grad_gain


def segment_forward(x_act, first_w, second_w, gain_rows):
    kept_list = []
    for layer_idx in range(first_w.shape[0]):
        kept_list.append(x_act)
        x_act = layer_forward(x_act, first_w[layer_idx], second_w[layer_idx], gain_rows[layer_idx])
    return x_act, jnp.stack(kept_list)


def segment_backward(kept_inputs, grad_h, first_w, second_w, gain_rows, grad_sums):
    layer_count = first_w.shape[0]
    first_list = [None] * layer_count
    second_list = [None] * layer_count
    gain_list = [None] * layer_count
    for layer_idx in reversed(range(layer_count)):
        grad_h, grad_first, grad_second, grad_gain = layer_backward(
            kept_inputs[layer_idx], grad_h, first_w[layer_idx], second_w[layer_idx], gain_rows[layer_idx])
        first_list[layer_idx] = grad_first
        second_list[layer_idx] = grad_second
        gain_list[layer_idx] = grad_gain
    new_sums = (grad_sums[0] + jnp.stack(first_list), grad_sums[1] + jnp.stack(second_list),
                grad_sums[2] + jnp.stack(gain_list))
    return grad_h, new_sums


def store_inputs(buffer_all, kept_inputs, mb_index, is_valid):
    old_rows = lax.dynamic_index_in_dim(buffer_all, mb_index, 1, keepdims=False)
    return lax.dynamic_update_index_in_dim(buffer_all, jnp.where(is_valid, kept_inputs, old_rows), mb_index, 1)


def solution(mesh):
    stages = mesh.shape['stage']
    down_perm = [(src_idx, src_idx + 1) for src_idx in range(stages - 1)]
    up_perm = [(src_idx + 1, src_idx) for src_idx in range(stages - 1)]

    def device_step(tokens, targets, w_in, w_out, norm_gains):
        stage_idx = lax.axis_index('stage')
        micro_count, tokens_mb, d_model = tokens.shape
        d_ff = w_in.shape[2]
        segment = w_in.shape[0] // 2
        tick_count = micro_count + 2 * stages - 1
        is_first = stage_idx == 0
        is_last = stage_idx == stages - 1
        up_offset = 2 * stages - 1 - stage_idx
        down_weights = (w_in[:segment], w_out[:segment], norm_gains[:segment])
        up_weights = (w_in[segment:], w_out[segment:], norm_gains[segment:])
        zero_act = jnp.zeros((tokens_mb, d_model), jnp.bfloat16)
        zero_saved = jnp.zeros((segment,) + tokens.shape, jnp.bfloat16)

        def run_down(x_act):
            return segment_forward(x_act, down_weights[0], down_weights[1], down_weights[2])

        def run_up(x_act):
            return segment_forward(x_act, up_weights[0], up_weights[1], up_weights[2])

        def skip_forward(x_act):
            return x_act, jnp.zeros((segment, tokens_mb, d_model), jnp.bfloat16)

        def forward_tick(loop_state, tick_idx):
            in_down, in_up, saved_down, saved_up, finals = loop_state
            mb_down = tick_idx - stage_idx
            mb_up = tick_idx - up_offset
            ok_down = (mb_down >= 0) & (mb_down < micro_count)
            ok_up = (mb_up >= 0) & (mb_up < micro_count)
            idx_down = jnp.clip(mb_down, 0, micro_count - 1)
            idx_up = jnp.clip(mb_up, 0, micro_count - 1)
            in_down = jnp.where(is_first, lax.dynamic_index_in_dim(tokens, idx_down, 0, keepdims=False), in_down)
            out_down, kept_down = lax.cond(ok_down, run_down, skip_forward, in_down)
            out_up, kept_up = lax.cond(ok_up, run_up, skip_forward, in_up)
            saved_down = store_inputs(saved_down, kept_down, idx_down, ok_down)
            saved_up = store_inputs(saved_up, kept_up, idx_up, ok_up)
            old_final = lax.dynamic_index_in_dim(finals, idx_up, 0, keepdims=False)
            finals = lax.dynamic_update_index_in_dim(
                finals, jnp.where(ok_up & is_first, out_up, old_final), idx_up, 0)
            recv_down = lax.ppermute(out_down, 'stage', down_perm)
            recv_up = lax.ppermute(out_up, 'stage', up_perm)
            next_up = jnp.where(is_last, out_down, recv_up)
            return (recv_down, next_up, saved_down, saved_up, finals), None

        fwd_init = (zero_act, zero_act, zero_saved, zero_saved, jnp.zeros(tokens.shape, jnp.bfloat16))
        fwd_state, _ = lax.scan(forward_tick, fwd_init, jnp.arange(tick_count))
        saved_down, saved_up, finals = fwd_state[2], fwd_state[3], fwd_state[4]
        error_f32 = finals.astype(jnp.float32) - targets.astype(jnp.float32)
        seed_grads = (error_f32 * (2.0 / (micro_count * tokens_mb))).astype(jnp.bfloat16)
        sse_local = jnp.where(is_first, jnp.sum(error_f32 * error_f32), 0.0)
        loss_value = lax.psum(sse_local, 'stage') / (micro_count * tokens_mb * d_model)

        def run_down_back(operand):
            return segment_backward(operand[1], operand[0], down_weights[0], down_weights[1],
                                    down_weights[2], operand[2])

        def run_up_back(operand):
            return segment_backward(operand[1], operand[0], up_weights[0], up_weights[1],
                                    up_weights[2], operand[2])

        def skip_backward(operand):
            return jnp.zeros_like(operand[0]), operand[2]

        def backward_tick(loop_state, tick_idx):
            grad_up_in, grad_down_in, sums_up, sums_down = loop_state
            mb_up = tick_idx - stage_idx
            mb_down = tick_idx - up_offset
            ok_up = (mb_up >= 0) & (mb_up < micro_count)
            ok_down = (mb_down >= 0) & (mb_down < micro_count)
            idx_up = jnp.clip(mb_up, 0, micro_count - 1)
            idx_down = jnp.clip(mb_down, 0, micro_count - 1)
            grad_up_in = jnp.where(is_first, lax.dynamic_index_in_dim(seed_grads, idx_up, 0, keepdims=False),
                                   grad_up_in)
            kept_up = lax.dynamic_index_in_dim(saved_up, idx_up, 1, keepdims=False)
            kept_down = lax.dynamic_index_in_dim(saved_down, idx_down, 1, keepdims=False)
            grad_up_out, sums_up = lax.cond(ok_up, run_up_back, skip_backward, (grad_up_in, kept_up, sums_up))
            grad_down_out, sums_down = lax.cond(ok_down, run_down_back, skip_backward,
                                                (grad_down_in, kept_down, sums_down))
            recv_up = lax.ppermute(grad_up_out, 'stage', down_perm)
            recv_down = lax.ppermute(grad_down_out, 'stage', up_perm)
            next_down = jnp.where(is_last, grad_up_out, recv_down)
            return (recv_up, next_down, sums_up, sums_down), None

        zero_sums = (jnp.zeros((segment, d_model, d_ff), jnp.float32),
                     jnp.zeros((segment, d_ff, d_model), jnp.float32),
                     jnp.zeros((segment, d_model), jnp.float32))
        back_init = (zero_act, zero_act, zero_sums, zero_sums)
        back_state, _ = lax.scan(backward_tick, back_init, jnp.arange(tick_count))
        sums_up, sums_down = back_state[2], back_state[3]
        grad_w_in = jnp.concatenate([sums_down[0], sums_up[0]], axis=0)
        grad_w_out = jnp.concatenate([sums_down[1], sums_up[1]], axis=0)
        grad_gains = jnp.concatenate([sums_down[2], sums_up[2]], axis=0)
        return grad_w_in, grad_w_out, grad_gains, loss_value.reshape(1)

    block_spec = P(('dp', 'stage'))
    return jax.shard_map(device_step, mesh=mesh,
                         in_specs=(P('dp'), P('dp'), P('stage'), P('stage'), P('stage')),
                         out_specs=(block_spec, block_spec, block_spec, P('dp')),
                         check_vma=False)
```

profile of v0, /device:TPU:0, one launch (start us, length us, event | category | flops | bytes accessed | tf_op | source)
XLA Modules:
  0.0 2483.4 jit_solution(16732147559281703422)
XLA Ops:
  20.7 789.1 %while.47 = (s32[]{:T(128)}, bf16[256,512]{1,0:T(8,128)(2,1)S(1)}, bf16[256,512]{1,0:T(8,128)(2,1)S(1)}, bf16[1,32,256,512]{3,2,1,0:T(8,128)(2,1)}, bf16[1,32,25...) while((s32[]{:T(128)}, bf16[256,512]{1,0:T(8,128)(2,1)S(1)}, ...), condition=%wide.region_7.8_spmd.clone, body=%wide.region_0.7_spmd.clone.sunk | while | flops 2160329216 | bytes 18100776 | solution.py:119
  831.1 1628.8 %while.48 = (s32[]{:T(128)}, bf16[256,512]{1,0:T(8,128)(2,1)S(1)}, bf16[256,512]{1,0:T(8,128)(2,1)S(1)}, f32[1,512,2048]{2,1,0:T(8,128)}, f32[1,2048,512]{2,1,0:...) while((s32[]{:T(128)}, bf16[256,512]{1,0:T(8,128)(2,1)S(1)}, ...), condition=%wide.region_19.20_spmd.clone, body=%wide.region_8.19_spmd.clone.sunk | while | flops 5411048448 | bytes 218162208 | solution.py:161
  1005.7 52.7 %collective-permute-start.2 = (bf16[256,512]{1,0:T(8,128)(2,1)S(1)}, bf16[256,512]{1,0:T(8,128)(2,1)S(1)}, u32[]{:S(2)}, u32[]{:S(2)}) collective-permute-start(bf16[256,512]{1,0:T(8,128)(2,1)S(1)} %get-tuple-element.971), channel_id=1, source_target_pairs={{0,1},{1,2},{2,3},{4,5},{5,6},{6,7},{8,9},{9,10},{10,11},{12,13},{... | collective-permute-start | bytes 786440 | tf_op jit(solution)/shard_map/while/body/eval_jaxpr/ppermute | solution.py:152
  1060.7 18.2 conditional.15
  1106.8 18.2 conditional.15
  1152.8 18.2 conditional.15
  1198.9 18.2 conditional.15
  1245.0 18.2 conditional.15
  1291.0 18.2 conditional.15
  1337.1 18.2 conditional.15
  1383.1 18.2 conditional.15
  1429.2 18.2 conditional.15
  1475.2 18.2 conditional.15
  1521.3 18.2 conditional.15
  1567.3 18.2 conditional.15
  1613.4 18.2 conditional.15
  1659.5 18.2 conditional.15
  1705.5 18.2 conditional.15
  1751.6 18.2 conditional.15
  1797.6 18.2 conditional.15
  1843.7 18.2 conditional.15
  1889.7 18.2 conditional.15
  1935.8 18.2 conditional.15
  1981.8 18.2 conditional.15
  2027.9 18.2 conditional.15
  2073.9 18.2 conditional.15
  2166.1 18.2 conditional.15
  2212.1 18.2 conditional.15
  2232.3 23.5 collective-permute-start.2
  2258.2 18.2 conditional.15
  2308.2 23.5 collective-permute-start.2
  2384.0 19.3 collective-permute-start.2
  (2380 shorter events, 3129.3 us)
Async XLA Ops:
  903.7 25.5 %collective-permute-start.3 = (bf16[256,512]{1,0:T(8,128)(2,1)S(1)}, bf16[256,512]{1,0:T(8,128)(2,1)S(1)}, u32[]{:S(2)}, u32[]{:S(2)}) collective-permute-start(bf16[256,512]{1,0:T(8,128)(2,1)S(1)} %get-tuple-element.972), channel_id=1, source_target_pairs={{1,0},{2,1},{3,2},{5,4},{6,5},{7,6},{9,8},{10,9},{11,10},{13,12},{... | collective-permute-start | bytes 786440 | tf_op jit(solution)/shard_map/while/body/eval_jaxpr/ppermute | solution.py:153
  931.7 25.4 %collective-permute-start.3 = (bf16[256,512]{1,0:T(8,128)(2,1)S(1)}, bf16[256,512]{1,0:T(8,128)(2,1)S(1)}, u32[]{:S(2)}, u32[]{:S(2)}) collective-permute-start(bf16[256,512]{1,0:T(8,128)(2,1)S(1)} %get-tuple-element.972), channel_id=1, source_target_pairs={{1,0},{2,1},{3,2},{5,4},{6,5},{7,6},{9,8},{10,9},{11,10},{13,12},{... | collective-permute-start | bytes 786440 | tf_op jit(solution)/shard_map/while/body/eval_jaxpr/ppermute | solution.py:153
  959.5 25.4 %collective-permute-start.3 = (bf16[256,512]{1,0:T(8,128)(2,1)S(1)}, bf16[256,512]{1,0:T(8,128)(2,1)S(1)}, u32[]{:S(2)}, u32[]{:S(2)}) collective-permute-start(bf16[256,512]{1,0:T(8,128)(2,1)S(1)} %get-tuple-element.972), channel_id=1, source_target_pairs={{1,0},{2,1},{3,2},{5,4},{6,5},{7,6},{9,8},{10,9},{11,10},{13,12},{... | collective-permute-start | bytes 786440 | tf_op jit(solution)/shard_map/while/body/eval_jaxpr/ppermute | solution.py:153
  987.4 70.9 %collective-permute-start.3 = (bf16[256,512]{1,0:T(8,128)(2,1)S(1)}, bf16[256,512]{1,0:T(8,128)(2,1)S(1)}, u32[]{:S(2)}, u32[]{:S(2)}) collective-permute-start(bf16[256,512]{1,0:T(8,128)(2,1)S(1)} %get-tuple-element.972), channel_id=1, source_target_pairs={{1,0},{2,1},{3,2},{5,4},{6,5},{7,6},{9,8},{10,9},{11,10},{13,12},{... | collective-permute-start | bytes 786440 | tf_op jit(solution)/shard_map/while/body/eval_jaxpr/ppermute | solution.py:153
  1005.7 53.8 %collective-permute-start.2 = (bf16[256,512]{1,0:T(8,128)(2,1)S(1)}, bf16[256,512]{1,0:T(8,128)(2,1)S(1)}, u32[]{:S(2)}, u32[]{:S(2)}) collective-permute-start(bf16[256,512]{1,0:T(8,128)(2,1)S(1)} %get-tuple-element.971), channel_id=1, source_target_pairs={{0,1},{1,2},{2,3},{4,5},{5,6},{6,7},{8,9},{9,10},{10,11},{12,13},{... | collective-permute-start | bytes 786440 | tf_op jit(solution)/shard_map/while/body/eval_jaxpr/ppermute | solution.py:152
  1079.0 25.5 %collective-permute-start.3 = (bf16[256,512]{1,0:T(8,128)(2,1)S(1)}, bf16[256,512]{1,0:T(8,128)(2,1)S(1)}, u32[]{:S(2)}, u32[]{:S(2)}) collective-permute-start(bf16[256,512]{1,0:T(8,128)(2,1)S(1)} %get-tuple-element.972), channel_id=1, source_target_pairs={{1,0},{2,1},{3,2},{5,4},{6,5},{7,6},{9,8},{10,9},{11,10},{13,12},{... | collective-permute-start | bytes 786440 | tf_op jit(solution)/shard_map/while/body/eval_jaxpr/ppermute | solution.py:153
  1125.0 25.5 %collective-permute-start.3 = (bf16[256,512]{1,0:T(8,128)(2,1)S(1)}, bf16[256,512]{1,0:T(8,128)(2,1)S(1)}, u32[]{:S(2)}, u32[]{:S(2)}) collective-permute-start(bf16[256,512]{1,0:T(8,128)(2,1)S(1)} %get-tuple-element.972), channel_id=1, source_target_pairs={{1,0},{2,1},{3,2},{5,4},{6,5},{7,6},{9,8},{10,9},{11,10},{13,12},{... | collective-permute-start | bytes 786440 | tf_op jit(solution)/shard_map/while/body/eval_jaxpr/ppermute | solution.py:153
  1171.1 25.5 %collective-permute-start.3 = (bf16[256,512]{1,0:T(8,128)(2,1)S(1)}, bf16[256,512]{1,0:T(8,128)(2,1)S(1)}, u32[]{:S(2)}, u32[]{:S(2)}) collective-permute-start(bf16[256,512]{1,0:T(8,128)(2,1)S(1)} %get-tuple-element.972), channel_id=1, source_target_pairs={{1,0},{2,1},{3,2},{5,4},{6,5},{7,6},{9,8},{10,9},{11,10},{13,12},{... | collective-permute-start | bytes 786440 | tf_op jit(solution)/shard_map/while/body/eval_jaxpr/ppermute | solution.py:153
  1217.1 25.5 %collective-permute-start.3 = (bf16[256,512]{1,0:T(8,128)(2,1)S(1)}, bf16[256,512]{1,0:T(8,128)(2,1)S(1)}, u32[]{:S(2)}, u32[]{:S(2)}) collective-permute-start(bf16[256,512]{1,0:T(8,128)(2,1)S(1)} %get-tuple-element.972), channel_id=1, source_target_pairs={{1,0},{2,1},{3,2},{5,4},{6,5},{7,6},{9,8},{10,9},{11,10},{13,12},{... | collective-permute-start | bytes 786440 | tf_op jit(solution)/shard_map/while/body/eval_jaxpr/ppermute | solution.py:153
  1263.2 25.5 %collective-permute-start.3 = (bf16[256,512]{1,0:T(8,128)(2,1)S(1)}, bf16[256,512]{1,0:T(8,128)(2,1)S(1)}, u32[]{:S(2)}, u32[]{:S(2)}) collective-permute-start(bf16[256,512]{1,0:T(8,128)(2,1)S(1)} %get-tuple-element.972), channel_id=1, source_target_pairs={{1,0},{2,1},{3,2},{5,4},{6,5},{7,6},{9,8},{10,9},{11,10},{13,12},{... | collective-permute-start | bytes 786440 | tf_op jit(solution)/shard_map/while/body/eval_jaxpr/ppermute | solution.py:153
  1309.2 25.5 %collective-permute-start.3 = (bf16[256,512]{1,0:T(8,128)(2,1)S(1)}, bf16[256,512]{1,0:T(8,128)(2,1)S(1)}, u32[]{:S(2)}, u32[]{:S(2)}) collective-permute-start(bf16[256,512]{1,0:T(8,128)(2,1)S(1)} %get-tuple-element.972), channel_id=1, source_target_pairs={{1,0},{2,1},{3,2},{5,4},{6,5},{7,6},{9,8},{10,9},{11,10},{13,12},{... | collective-permute-start | bytes 786440 | tf_op jit(solution)/shard_map/while/body/eval_jaxpr/ppermute | solution.py:153
  1355.3 25.5 %collective-permute-start.3 = (bf16[256,512]{1,0:T(8,128)(2,1)S(1)}, bf16[256,512]{1,0:T(8,128)(2,1)S(1)}, u32[]{:S(2)}, u32[]{:S(2)}) collective-permute-start(bf16[256,512]{1,0:T(8,128)(2,1)S(1)} %get-tuple-element.972), channel_id=1, source_target_pairs={{1,0},{2,1},{3,2},{5,4},{6,5},{7,6},{9,8},{10,9},{11,10},{13,12},{... | collective-permute-start | bytes 786440 | tf_op jit(solution)/shard_map/while/body/eval_jaxpr/ppermute | solution.py:153
  1401.3 25.5 %collective-permute-start.3 = (bf16[256,512]{1,0:T(8,128)(2,1)S(1)}, bf16[256,512]{1,0:T(8,128)(2,1)S(1)}, u32[]{:S(2)}, u32[]{:S(2)}) collective-permute-start(bf16[256,512]{1,0:T(8,128)(2,1)S(1)} %get-tuple-element.972), channel_id=1, source_target_pairs={{1,0},{2,1},{3,2},{5,4},{6,5},{7,6},{9,8},{10,9},{11,10},{13,12},{... | collective-permute-start | bytes 786440 | tf_op jit(solution)/shard_map/while/body/eval_jaxpr/ppermute | solution.py:153
  1447.4 25.5 %collective-permute-start.3 = (bf16[256,512]{1,0:T(8,128)(2,1)S(1)}, bf16[256,512]{1,0:T(8,128)(2,1)S(1)}, u32[]{:S(2)}, u32[]{:S(2)}) collective-permute-start(bf16[256,512]{1,0:T(8,128)(2,1)S(1)} %get-tuple-element.972), channel_id=1, source_target_pairs={{1,0},{2,1},{3,2},{5,4},{6,5},{7,6},{9,8},{10,9},{11,10},{13,12},{... | collective-permute-start | bytes 786440 | tf_op jit(solution)/shard_map/while/body/eval_jaxpr/ppermute | solution.py:153
  1493.5 25.5 %collective-permute-start.3 = (bf16[256,512]{1,0:T(8,128)(2,1)S(1)}, bf16[256,512]{1,0:T(8,128)(2,1)S(1)}, u32[]{:S(2)}, u32[]{:S(2)}) collective-permute-start(bf16[256,512]{1,0:T(8,128)(2,1)S(1)} %get-tuple-element.972), channel_id=1, source_target_pairs={{1,0},{2,1},{3,2},{5,4},{6,5},{7,6},{9,8},{10,9},{11,10},{13,12},{... | collective-permute-start | bytes 786440 | tf_op jit(solution)/shard_map/while/body/eval_jaxpr/ppermute | solution.py:153
  1539.5 25.5 %collective-permute-start.3 = (bf16[256,512]{1,0:T(8,128)(2,1)S(1)}, bf16[256,512]{1,0:T(8,128)(2,1)S(1)}, u32[]{:S(2)}, u32[]{:S(2)}) collective-permute-start(bf16[256,512]{1,0:T(8,128)(2,1)S(1)} %get-tuple-element.972), channel_id=1, source_target_pairs={{1,0},{2,1},{3,2},{5,4},{6,5},{7,6},{9,8},{10,9},{11,10},{13,12},{... | collective-permute-start | bytes 786440 | tf_op jit(solution)/shard_map/while/body/eval_jaxpr/ppermute | solution.py:153
  1585.6 25.5 %collective-permute-start.3 = (bf16[256,512]{1,0:T(8,128)(2,1)S(1)}, bf16[256,512]{1,0:T(8,128)(2,1)S(1)}, u32[]{:S(2)}, u32[]{:S(2)}) collective-permute-start(bf16[256,512]{1,0:T(8,128)(2,1)S(1)} %get-tuple-element.972), channel_id=1, source_target_pairs={{1,0},{2,1},{3,2},{5,4},{6,5},{7,6},{9,8},{10,9},{11,10},{13,12},{... | collective-permute-start | bytes 786440 | tf_op jit(solution)/shard_map/while/body/eval_jaxpr/ppermute | solution.py:153
  1631.6 25.5 %collective-permute-start.3 = (bf16[256,512]{1,0:T(8,128)(2,1)S(1)}, bf16[256,512]{1,0:T(8,128)(2,1)S(1)}, u32[]{:S(2)}, u32[]{:S(2)}) collective-permute-start(bf16[256,512]{1,0:T(8,128)(2,1)S(1)} %get-tuple-element.972), channel_id=1, source_target_pairs={{1,0},{2,1},{3,2},{5,4},{6,5},{7,6},{9,8},{10,9},{11,10},{13,12},{... | collective-permute-start | bytes 786440 | tf_op jit(solution)/shard_map/while/body/eval_jaxpr/ppermute | solution.py:153
  1677.7 25.5 %collective-permute-start.3 = (bf16[256,512]{1,0:T(8,128)(2,1)S(1)}, bf16[256,512]{1,0:T(8,128)(2,1)S(1)}, u32[]{:S(2)}, u32[]{:S(2)}) collective-permute-start(bf16[256,512]{1,0:T(8,128)(2,1)S(1)} %get-tuple-element.972), channel_id=1, source_target_pairs={{1,0},{2,1},{3,2},{5,4},{6,5},{7,6},{9,8},{10,9},{11,10},{13,12},{... | collective-permute-start | bytes 786440 | tf_op jit(solution)/shard_map/while/body/eval_jaxpr/ppermute | solution.py:153
  1723.7 25.5 %collective-permute-start.3 = (bf16[256,512]{1,0:T(8,128)(2,1)S(1)}, bf16[256,512]{1,0:T(8,128)(2,1)S(1)}, u32[]{:S(2)}, u32[]{:S(2)}) collective-permute-start(bf16[256,512]{1,0:T(8,128)(2,1)S(1)} %get-tuple-element.972), channel_id=1, source_target_pairs={{1,0},{2,1},{3,2},{5,4},{6,5},{7,6},{9,8},{10,9},{11,10},{13,12},{... | collective-permute-start | bytes 786440 | tf_op jit(solution)/shard_map/while/body/eval_jaxpr/ppermute | solution.py:153
  1769.8 25.5 %collective-permute-start.3 = (bf16[256,512]{1,0:T(8,128)(2,1)S(1)}, bf16[256,512]{1,0:T(8,128)(2,1)S(1)}, u32[]{:S(2)}, u32[]{:S(2)}) collective-permute-start(bf16[256,512]{1,0:T(8,128)(2,1)S(1)} %get-tuple-element.972), channel_id=1, source_target_pairs={{1,0},{2,1},{3,2},{5,4},{6,5},{7,6},{9,8},{10,9},{11,10},{13,12},{... | collective-permute-start | bytes 786440 | tf_op jit(solution)/shard_map/while/body/eval_jaxpr/ppermute | solution.py:153
  1815.8 25.5 %collective-permute-start.3 = (bf16[256,512]{1,0:T(8,128)(2,1)S(1)}, bf16[256,512]{1,0:T(8,128)(2,1)S(1)}, u32[]{:S(2)}, u32[]{:S(2)}) collective-permute-start(bf16[256,512]{1,0:T(8,128)(2,1)S(1)} %get-tuple-element.972), channel_id=1, source_target_pairs={{1,0},{2,1},{3,2},{5,4},{6,5},{7,6},{9,8},{10,9},{11,10},{13,12},{... | collective-permute-start | bytes 786440 | tf_op jit(solution)/shard_map/while/body/eval_jaxpr/ppermute | solution.py:153
  1861.9 25.5 %collective-permute-start.3 = (bf16[256,512]{1,0:T(8,128)(2,1)S(1)}, bf16[256,512]{1,0:T(8,128)(2,1)S(1)}, u32[]{:S(2)}, u32[]{:S(2)}) collective-permute-start(bf16[256,512]{1,0:T(8,128)(2,1)S(1)} %get-tuple-element.972), channel_id=1, source_target_pairs={{1,0},{2,1},{3,2},{5,4},{6,5},{7,6},{9,8},{10,9},{11,10},{13,12},{... | collective-permute-start | bytes 786440 | tf_op jit(solution)/shard_map/while/body/eval_jaxpr/ppermute | solution.py:153
  1907.9 25.5 %collective-permute-start.3 = (bf16[256,512]{1,0:T(8,128)(2,1)S(1)}, bf16[256,512]{1,0:T(8,128)(2,1)S(1)}, u32[]{:S(2)}, u32[]{:S(2)}) collective-permute-start(bf16[256,512]{1,0:T(8,128)(2,1)S(1)} %get-tuple-element.972), channel_id=1, source_target_pairs={{1,0},{2,1},{3,2},{5,4},{6,5},{7,6},{9,8},{10,9},{11,10},{13,12},{... | collective-permute-start | bytes 786440 | tf_op jit(solution)/shard_map/while/body/eval_jaxpr/ppermute | solution.py:153
  1954.0 25.5 %collective-permute-start.3 = (bf16[256,512]{1,0:T(8,128)(2,1)S(1)}, bf16[256,512]{1,0:T(8,128)(2,1)S(1)}, u32[]{:S(2)}, u32[]{:S(2)}) collective-permute-start(bf16[256,512]{1,0:T(8,128)(2,1)S(1)} %get-tuple-element.972), channel_id=1, source_target_pairs={{1,0},{2,1},{3,2},{5,4},{6,5},{7,6},{9,8},{10,9},{11,10},{13,12},{... | collective-permute-start | bytes 786440 | tf_op jit(solution)/shard_map/while/body/eval_jaxpr/ppermute | solution.py:153
  2000.1 25.5 %collective-permute-start.3 = (bf16[256,512]{1,0:T(8,128)(2,1)S(1)}, bf16[256,512]{1,0:T(8,128)(2,1)S(1)}, u32[]{:S(2)}, u32[]{:S(2)}) collective-permute-start(bf16[256,512]{1,0:T(8,128)(2,1)S(1)} %get-tuple-element.972), channel_id=1, source_target_pairs={{1,0},{2,1},{3,2},{5,4},{6,5},{7,6},{9,8},{10,9},{11,10},{13,12},{... | collective-permute-start | bytes 786440 | tf_op jit(solution)/shard_map/while/body/eval_jaxpr/ppermute | solution.py:153
  2046.1 25.5 %collective-permute-start.3 = (bf16[256,512]{1,0:T(8,128)(2,1)S(1)}, bf16[256,512]{1,0:T(8,128)(2,1)S(1)}, u32[]{:S(2)}, u32[]{:S(2)}) collective-permute-start(bf16[256,512]{1,0:T(8,128)(2,1)S(1)} %get-tuple-element.972), channel_id=1, source_target_pairs={{1,0},{2,1},{3,2},{5,4},{6,5},{7,6},{9,8},{10,9},{11,10},{13,12},{... | collective-permute-start | bytes 786440 | tf_op jit(solution)/shard_map/while/body/eval_jaxpr/ppermute | solution.py:153
  2092.2 25.5 %collective-permute-start.3 = (bf16[256,512]{1,0:T(8,128)(2,1)S(1)}, bf16[256,512]{1,0:T(8,128)(2,1)S(1)}, u32[]{:S(2)}, u32[]{:S(2)}) collective-permute-start(bf16[256,512]{1,0:T(8,128)(2,1)S(1)} %get-tuple-element.972), channel_id=1, source_target_pairs={{1,0},{2,1},{3,2},{5,4},{6,5},{7,6},{9,8},{10,9},{11,10},{13,12},{... | collective-permute-start | bytes 786440 | tf_op jit(solution)/shard_map/while/body/eval_jaxpr/ppermute | solution.py:153
  2138.2 25.5 %collective-permute-start.3 = (bf16[256,512]{1,0:T(8,128)(2,1)S(1)}, bf16[256,512]{1,0:T(8,128)(2,1)S(1)}, u32[]{:S(2)}, u32[]{:S(2)}) collective-permute-start(bf16[256,512]{1,0:T(8,128)(2,1)S(1)} %get-tuple-element.972), channel_id=1, source_target_pairs={{1,0},{2,1},{3,2},{5,4},{6,5},{7,6},{9,8},{10,9},{11,10},{13,12},{... | collective-permute-start | bytes 786440 | tf_op jit(solution)/shard_map/while/body/eval_jaxpr/ppermute | solution.py:153
  2184.3 25.5 %collective-permute-start.3 = (bf16[256,512]{1,0:T(8,128)(2,1)S(1)}, bf16[256,512]{1,0:T(8,128)(2,1)S(1)}, u32[]{:S(2)}, u32[]{:S(2)}) collective-permute-start(bf16[256,512]{1,0:T(8,128)(2,1)S(1)} %get-tuple-element.972), channel_id=1, source_target_pairs={{1,0},{2,1},{3,2},{5,4},{6,5},{7,6},{9,8},{10,9},{11,10},{13,12},{... | collective-permute-start | bytes 786440 | tf_op jit(solution)/shard_map/while/body/eval_jaxpr/ppermute | solution.py:153
  2230.3 25.5 %collective-permute-start.3 = (bf16[256,512]{1,0:T(8,128)(2,1)S(1)}, bf16[256,512]{1,0:T(8,128)(2,1)S(1)}, u32[]{:S(2)}, u32[]{:S(2)}) collective-permute-start(bf16[256,512]{1,0:T(8,128)(2,1)S(1)} %get-tuple-element.972), channel_id=1, source_target_pairs={{1,0},{2,1},{3,2},{5,4},{6,5},{7,6},{9,8},{10,9},{11,10},{13,12},{... | collective-permute-start | bytes 786440 | tf_op jit(solution)/shard_map/while/body/eval_jaxpr/ppermute | solution.py:153
  2306.2 25.5 %collective-permute-start.3 = (bf16[256,512]{1,0:T(8,128)(2,1)S(1)}, bf16[256,512]{1,0:T(8,128)(2,1)S(1)}, u32[]{:S(2)}, u32[]{:S(2)}) collective-permute-start(bf16[256,512]{1,0:T(8,128)(2,1)S(1)} %get-tuple-element.972), channel_id=1, source_target_pairs={{1,0},{2,1},{3,2},{5,4},{6,5},{7,6},{9,8},{10,9},{11,10},{13,12},{... | collective-permute-start | bytes 786440 | tf_op jit(solution)/shard_map/while/body/eval_jaxpr/ppermute | solution.py:153
  (416 other events, 2368.3 us)
where the time goes:
time: 2500 us; the launch traced here: 2480 us
  matrix products  1080 us (43%)
  starting transfers between devices  631 us (25%)
  other arithmetic  319 us (13%)
  local copies, waits for them, and re-layouts  278 us (11%)
  loops' own time  121 us (5%)
  waiting for transfers between devices  42.4 us (2%)
    ppermute x39, starting transfers between devices, backward_tick(): recv_up = lax.ppermute(grad_up_out, 'stage', down_perm)  354 us
    dot_general x64, matrix products, layer_backward(): jnp.einsum('tf,df->td', grad_pre, first_w, preferred_element_type=jnp.flo...  256 us
    dot_general x64, matrix products, layer_forward(): out_f32 = jnp.dot(hidden, second_w, preferred_element_type=jnp.float32)  245 us
    ppermute x39, starting transfers between devices, forward_tick(): recv_down = lax.ppermute(out_down, 'stage', down_perm)  177 us
    dot_general x64, matrix products, layer_backward(): jnp.einsum('td,fd->tf', grad_h, second_w, preferred_element_type=jnp.floa...  167 us
    dot_general x64, matrix products, layer_backward(): pre_act = jnp.dot(normed, first_w, preferred_element_type=jnp.float32)  161 us
    dot_general x64, matrix products, layer_backward(): jnp.einsum('td,tf->df', normed, grad_pre, preferred_element_type=jnp.floa...  138 us
    dot_general x64, matrix products, layer_backward(): jnp.einsum('tf,td->fd', hidden, grad_h, preferred_element_type=jnp.float32)  113 us
  transfers between devices with their start and end apart: 156, of which 39 were waited for; matrix products, arithmetic and copies ran while one was open for 34% of the time, Pallas kernels for 0%

commit v1 on v0

v1 whole, which is shorter than its diff:
```python
import functools

import jax
import jax.numpy as jnp
from jax import lax
from jax.experimental import pallas as pl
from jax.experimental.pallas import tpu as pltpu
from jax.sharding import PartitionSpec as P

EPSILON = 1e-6
MESH = pl.DeviceIdType.MESH
F32 = jnp.float32
BF16 = jnp.bfloat16
C0 = 0.7978845608028654
C1 = C0 * 0.044715
RING = 8
TOK_AHEAD = 4
TGT_SLOTS = 4
CHUNK_F = 512
CHUNK_B = 512


def dot(lhs, rhs):
    return jnp.dot(lhs, rhs, preferred_element_type=F32)


def dot_t(lhs, rhs):
    return lax.dot_general(lhs, rhs, (((1,), (1,)), ((), ())), preferred_element_type=F32)


def gate(a):
    sq = a * a
    z = a * (C0 + C1 * sq)
    return 0.5 + 0.5 * jnp.tanh(z), sq


def kernel(n_stage, n_micro, tok_hbm, tgt_hbm, wi_hbm, wo_hbm, gain_ref,
           gwi_hbm, gwo_hbm, gg_ref, loss_ref,
           wi, wo, agi, ago, gg, xs, dhs, of, ob, tg, da_s, u_s, sse, loss_src, loss_dst,
           w_sem, out_sem, tg_sem, rx_sem, rd_sem, sf_sem, sb_sem, free_sem, lsend_sem, lrecv_sem):
    stage = lax.axis_index('stage')
    last = n_stage - 1
    is_first = stage == 0
    is_last = stage == last
    tokens_mb, d_model = xs.shape[2], xs.shape[3]
    d_ff = wi.shape[2]
    seed_scale = 2.0 / (n_micro * tokens_mb)

    barrier = pltpu.get_barrier_semaphore()
    for hop in range(1, n_stage):
        pl.semaphore_signal(barrier, inc=1, device_id={'stage': lax.rem(stage + hop, n_stage)},
                            device_id_type=MESH)
    pl.semaphore_wait(barrier, n_stage - 1)

    def weight_copies(layer):
        return (pltpu.make_async_copy(wi_hbm.at[layer], wi.at[layer], w_sem.at[layer, 0]),
                pltpu.make_async_copy(wo_hbm.at[layer], wo.at[layer], w_sem.at[layer, 1]))

    def token_copy(mb):
        return pltpu.make_async_copy(tok_hbm.at[mb], xs.at[0, mb], rx_sem.at[0, mb])

    def target_copy(mb):
        slot = lax.rem(mb, TGT_SLOTS)
        return pltpu.make_async_copy(tgt_hbm.at[mb], tg.at[slot], tg_sem.at[slot])

    def out_copies(layer):
        return (pltpu.make_async_copy(agi.at[layer], gwi_hbm.at[layer], out_sem.at[layer, 0]),
                pltpu.make_async_copy(ago.at[layer], gwo_hbm.at[layer], out_sem.at[layer, 1]))

    for copy in weight_copies(0):
        copy.start()

    @pl.when(is_first)
    def _():
        for mb in range(TOK_AHEAD):
            token_copy(mb).start()

    for copy in weight_copies(1):
        copy.start()

    @pl.when(is_first)
    def _():
        for mb in range(TGT_SLOTS):
            target_copy(mb).start()

    @pl.loop(0, 2 * d_model // 8)
    def _(i):
        layer, row = i // (d_model // 8), lax.rem(i, d_model // 8)
        rows = pl.ds(pl.multiple_of(row * 8, 8), 8)
        agi[layer, rows, :] = jnp.zeros((8, d_ff), F32)
        ago[layer, rows, :] = jnp.zeros((8, d_ff), F32)

    gg[...] = jnp.zeros_like(gg)
    sse[...] = jnp.zeros_like(sse)
    for layer in range(2):
        for copy in weight_copies(layer):
            copy.wait()

    def gain_of(layer):
        return jnp.where(layer == 0, gain_ref[0:1, :], gain_ref[1:2, :])

    def fold(rows):
        return jnp.sum(rows.reshape(rows.shape[0] // 8, 8, rows.shape[1]), axis=0)

    def forward(layer, mb):
        x = xs[layer, mb].astype(F32)
        inv = lax.rsqrt(jnp.mean(x * x, axis=-1, keepdims=True) + EPSILON)
        normed = (x * inv * gain_of(layer)).astype(BF16)
        total = x
        for c in range(d_ff // CHUNK_F):
            cols = pl.ds(c * CHUNK_F, CHUNK_F)
            a = dot(normed, wi[layer, :, cols])
            q, _ = gate(a)
            total = total + dot((a * q).astype(BF16), wo[layer, cols, :])
        return total.astype(BF16)

    def backward(layer, mb, slot):
        x = xs[layer, mb].astype(F32)
        gain = gain_of(layer)
        inv = lax.rsqrt(jnp.mean(x * x, axis=-1, keepdims=True) + EPSILON)
        xhat = x * inv
        normed = (xhat * gain).astype(BF16)
        dh = dhs[layer, slot]
        dn = None
        for c in range(d_ff // CHUNK_B):
            cols = pl.ds(c * CHUNK_B, CHUNK_B)
            a = dot(normed, wi[layer, :, cols])
            du = dot_t(dh, wo[layer, cols, :])
            q, sq = gate(a)
            u = a * q
            slope = q + u * (1.0 - q) * (2.0 * C0 + 6.0 * C1 * sq)
            da = (du * slope).astype(BF16)
            u_s[:, cols] = u.astype(BF16)
            da_s[:, cols] = da
            part = dot_t(da, wi[layer, :, cols])
            dn = part if dn is None else dn + part
        weighted = dn * gain
        proj = jnp.mean(weighted * xhat, axis=-1, keepdims=True)
        gg[layer] += fold(dn * xhat)
        return (dh.astype(F32) + inv * (weighted - xhat * proj)).astype(BF16)

    def weight_grads(layer, mb, slot):
        x = xs[layer, mb].astype(F32)
        inv = lax.rsqrt(jnp.mean(x * x, axis=-1, keepdims=True) + EPSILON)
        normed_t = (x * inv * gain_of(layer)).astype(BF16).T
        dh_t = dhs[layer, slot].T
        for c in range(d_ff // CHUNK_B):
            cols = pl.ds(c * CHUNK_B, CHUNK_B)
            agi[layer, :, cols] += dot(normed_t, da_s[:, cols])
            ago[layer, :, cols] += dot(dh_t, u_s[:, cols])

    def send_f(layer, mb, target):
        par = lax.rem(mb, 2)
        return pltpu.make_async_remote_copy(
            src_ref=of.at[layer, par], dst_ref=xs.at[layer, mb],
            send_sem=sf_sem.at[layer, par], recv_sem=rx_sem.at[layer, mb],
            device_id={'stage': target}, device_id_type=MESH)

    def send_b(layer, mb, target):
        par = lax.rem(mb, 2)
        slot = lax.rem(mb, RING)
        return pltpu.make_async_remote_copy(
            src_ref=ob.at[layer, par], dst_ref=dhs.at[layer, slot],
            send_sem=sb_sem.at[layer, par], recv_sem=rd_sem.at[layer, slot],
            device_id={'stage': target}, device_id_type=MESH)

    def forward_unit(layer, mb):
        down = layer == 0
        sends = jnp.where(down, stage < last, stage > 0)
        receives = jnp.where(down, True, stage < last)
        target = jnp.where(down, jnp.minimum(stage + 1, last), jnp.maximum(stage - 1, 0))
        par = lax.rem(mb, 2)

        @pl.when(down & is_first & (mb + TOK_AHEAD < n_micro))
        def _():
            token_copy(mb + TOK_AHEAD).start()

        @pl.when(receives)
        def _():
            send_f(layer, mb, target).wait_recv()

        @pl.when(sends & (mb >= 2))
        def _():
            send_f(layer, mb - 2, target).wait_send()

        of[layer, par] = forward(layer, mb)

        @pl.when(sends)
        def _():
            send_f(layer, mb, target).start()

        @pl.when(down & is_last)
        def _():
            xs[1, mb] = of[0, par]

        @pl.when(jnp.logical_not(down) & is_first)
        def _():
            target_copy(mb).wait()
            tslot = lax.rem(mb, TGT_SLOTS)
            err = of[1, par].astype(F32) - tg[tslot].astype(F32)
            dhs[1, lax.rem(mb, RING)] = (err * seed_scale).astype(BF16)
            sse[...] += fold(err * err)

            @pl.when(mb + TGT_SLOTS < n_micro)
            def _():
                target_copy(mb + TGT_SLOTS).start()

    def backward_unit(layer, mb):
        up = layer == 1
        sends = jnp.where(up, stage < last, stage > 0)
        receives = jnp.where(up, stage > 0, stage < last)
        target = jnp.where(up, jnp.minimum(stage + 1, last), jnp.maximum(stage - 1, 0))
        source = jnp.where(up, jnp.maximum(stage - 1, 0), jnp.minimum(stage + 1, last))
        par = lax.rem(mb, 2)
        slot = lax.rem(mb, RING)

        @pl.when(receives)
        def _():
            send_b(layer, mb, target).wait_recv()

        @pl.when(sends & (mb >= 2))
        def _():
            send_b(layer, mb - 2, target).wait_send()

        ob[layer, par] = backward(layer, mb, slot)

        @pl.when(sends & (mb >= RING))
        def _():
            pl.semaphore_wait(free_sem.at[layer], 1)

        @pl.when(sends)
        def _():
            send_b(layer, mb, target).start()

        @pl.when(up & is_last)
        def _():
            dhs[0, slot] = ob[1, par]

        weight_grads(layer, mb, slot)

        @pl.when(receives & (mb + RING < n_micro))
        def _():
            pl.semaphore_signal(free_sem.at[layer], inc=1, device_id={'stage': source}, device_id_type=MESH)

        @pl.when(mb == n_micro - 1)
        def _():
            for copy in out_copies(layer):
                copy.start()

    def loss_copy(peer):
        return pltpu.make_async_remote_copy(
            src_ref=loss_src, dst_ref=loss_dst, send_sem=lsend_sem.at[peer - 1], recv_sem=lrecv_sem.at[0],
            device_id={'stage': peer}, device_id_type=MESH)

    ticks = n_micro + 4 * last

    @pl.loop(0, ticks)
    def _(tick):
        @pl.loop(0, 2)
        def _(layer):
            mb = tick - jnp.where(layer == 0, stage, 2 * last - stage)

            @pl.when((mb >= 0) & (mb < n_micro))
            def _():
                forward_unit(layer, mb)

        @pl.when(is_first & (tick == n_micro - 1 + 2 * last))
        def _():
            total = jnp.sum(sse[...]) / (n_micro * tokens_mb * d_model)
            loss_src[...] = jnp.full(loss_src.shape, total, F32)
            for peer in range(1, n_stage):
                loss_copy(peer).start()

        @pl.loop(0, 2)
        def _(index):
            layer = 1 - index
            mb = tick - jnp.where(layer == 1, 2 * last + stage, 4 * last - stage)

            @pl.when((mb >= 0) & (mb < n_micro))
            def _():
                backward_unit(layer, mb)

    gg_ref[...] = jnp.sum(gg[...], axis=1)

    @pl.when(is_first)
    def _():
        for peer in range(1, n_stage):
            loss_copy(peer).wait_send()
        loss_ref[0, 0] = loss_src[0, 0]

    @pl.when(jnp.logical_not(is_first))
    def _():
        loss_copy(1).wait_recv()
        loss_ref[0, 0] = loss_dst[0, 0]

    for layer in range(2):
        f_sends = stage < last if layer == 0 else stage > 0
        b_sends = stage < last if layer == 1 else stage > 0
        f_target = jnp.minimum(stage + 1, last) if layer == 0 else jnp.maximum(stage - 1, 0)
        b_target = jnp.minimum(stage + 1, last) if layer == 1 else jnp.maximum(stage - 1, 0)

        @pl.when(f_sends)
        def _():
            for mb in (n_micro - 2, n_micro - 1):
                send_f(layer, mb, f_target).wait_send()

        @pl.when(b_sends)
        def _():
            for mb in (n_micro - 2, n_micro - 1):
                send_b(layer, mb, b_target).wait_send()

        for copy in out_copies(layer):
            copy.wait()


def solution(mesh):
    n_stage = mesh.shape['stage']

    def device_step(tokens, targets, w_in, w_out, norm_gains):
        n_micro, tokens_mb, d_model = tokens.shape
        d_ff = w_in.shape[2]
        any_spec = pl.BlockSpec(memory_space=pl.ANY)
        dma = pltpu.SemaphoreType.DMA
        grad_w_in, grad_w_out_t, grad_gains, loss = pl.pallas_call(
            functools.partial(kernel, n_stage, n_micro),
            out_shape=(jax.ShapeDtypeStruct((2, d_model, d_ff), F32),
                       jax.ShapeDtypeStruct((2, d_model, d_ff), F32),
                       jax.ShapeDtypeStruct((2, d_model), F32),
                       jax.ShapeDtypeStruct((1, 1), F32)),
            in_specs=[any_spec] * 4 + [pl.BlockSpec(memory_space=pltpu.VMEM)],
            out_specs=(any_spec, any_spec, pl.BlockSpec(memory_space=pltpu.VMEM),
                       pl.BlockSpec(memory_space=pltpu.SMEM)),
            scratch_shapes=[
                pltpu.VMEM((2, d_model, d_ff), BF16),
                pltpu.VMEM((2, d_ff, d_model), BF16),
                pltpu.VMEM((2, d_model, d_ff), F32),
                pltpu.VMEM((2, d_model, d_ff), F32),
                pltpu.VMEM((2, 8, d_model), F32),
                pltpu.VMEM((2, n_micro, tokens_mb, d_model), BF16),
                pltpu.VMEM((2, RING, tokens_mb, d_model), BF16),
                pltpu.VMEM((2, 2, tokens_mb, d_model), BF16),
                pltpu.VMEM((2, 2, tokens_mb, d_model), BF16),
                pltpu.VMEM((TGT_SLOTS, tokens_mb, d_model), BF16),
                pltpu.VMEM((tokens_mb, d_ff), BF16),
                pltpu.VMEM((tokens_mb, d_ff), BF16),
                pltpu.VMEM((8, d_model), F32),
                pltpu.VMEM((8, 128), F32),
                pltpu.VMEM((8, 128), F32),
                dma((2, 2)), dma((2, 2)), dma((TGT_SLOTS,)), dma((2, n_micro)), dma((2, RING)),
                dma((2, 2)), dma((2, 2)), pltpu.SemaphoreType.REGULAR((2,)),
                dma((n_stage - 1,)), dma((1,)),
            ],
            compiler_params=pltpu.CompilerParams(
                collective_id=0, has_side_effects=True, vmem_limit_bytes=67043328),
        )(tokens, targets, w_in, w_out, norm_gains)
        return grad_w_in, jnp.swapaxes(grad_w_out_t, 1, 2), grad_gains, loss.reshape(1)

    block_spec = P(('dp', 'stage'))
    return jax.shard_map(device_step, mesh=mesh,
                         in_specs=(P('dp'), P('dp'), P('stage'), P('stage'), P('stage')),
                         out_specs=(block_spec, block_spec, block_spec, P('dp')),
                         check_vma=False)
```

time: 2500 us -> 462 us (0.18)
  matrix products: 1080 us -> 0 us
  starting transfers between devices: 631 us -> 0 us
  Pallas kernels: 0 us -> 442 us
  other arithmetic: 319 us -> 0 us
  local copies, waits for them, and re-layouts: 278 us -> 17.2 us
  loops' own time: 121 us -> 0 us
  waiting for transfers between devices: 42.4 us -> 0 us
    dot_general x384 -> x0, matrix products: 1080 us -> none  [the longest x64 256 us: layer_backward(): jnp.einsum('tf,df->td', grad_pre, first_w, preferred_element_type=jnp.flo...]
    ppermute x156 -> x0, starting transfers between devices: 631 us -> none  [the longest x39 354 us: backward_tick(): recv_up = lax.ppermute(grad_up_out, 'stage', down_perm)]
    pallas_call x0 -> x1, Pallas kernels: none -> 442 us  [device_step(): pl.pallas_call(functools.partial(kernel, n_stage, n_micro), out_shape=(ja...]
    dynamic_slice x195 -> x0, local copies, waits for them, and re-layouts: 163 us -> none  [the longest x78 75.9 us: store_inputs(): old_rows = lax.dynamic_index_in_dim(buffer_all, mb_index, 1, keepdims=False)]
    another operation x158 -> x0, loops' own time: 121 us -> none  [the longest x1 58.2 us: device_step(): fwd_state, _ = lax.scan(forward_tick, fwd_init, jnp.arange(tick_count))]
    reduce_sum x129 -> x0, other arithmetic: 89 us -> none  [the longest x128 77.7 us: norm_scale(): jnp.mean(x_f32 * x_f32, axis=-1, keepdims=True) + EPSILON]
    cond x590 -> x0, local copies, waits for them, and re-layouts: 84.4 us -> none
    convert_element_type x64 -> x0, other arithmetic: 74.6 us -> none  [layer_backward(): grad_x = (grad_h.astype(jnp.float32) + grad_x_norm).astype(jnp.bfloat16)]
  transfers between devices with their start and end apart: 156 -> 0, of which waited for: 39 -> 0; matrix products, arithmetic and copies ran while one was open for 34% -> 0% of each run, Pallas kernels for 0% -> 0%
where the time goes in v1:
time: 462 us
  Pallas kernels  442 us (96%)
  local copies, waits for them, and re-layouts  17.2 us (4%)
    pallas_call x1, Pallas kernels, device_step(): pl.pallas_call(functools.partial(kernel, n_stage, n_micro), out_shape=(ja...  442 us
    unnamed x5, local copies, waits for them, and re-layouts  17.2 us

profile of v1, /device:TPU:0, one launch (start us, length us, event | category | flops | bytes accessed | tf_op | source)
XLA Modules:
  0.0 461.5 jit_solution(10651781477540726359)
XLA Ops:
  0.6 442.0 %shard_map.84 = (f32[2,512,2048]{2,1,0:T(8,128)}, f32[2,512,2048]{2,1,0:T(8,128)}, f32[2,512]{1,0:T(2,128)}, f32[1,1]{1,0:T(1,128)}) custom-call(bf16[32,256,512]{2,1,0:T(8,128)(2,1)} %tok_hbm.1, bf16[32,256,512]{2,1,0:T(8,128)(2,1)} %tgt_hbm.1, bf16[2,512,2048]{2,1,0:T(8,128)(2,1)} %wi_hbm.1, bf16[2,2048,512]{2,1,0:T(8,128)(2,1)} %wo_hbm.1, f32[2,512]{1,0:T(2,128)} %gain_ref.1), custom_call_target="tpu_custom_call" | custom-call | tf_op jit(solution)/shard_map/pallas_call | solution.py:324
  442.6 8.7 %copy.9 = f32[2,2048,512]{2,1,0:T(8,128)} copy(f32[2,2048,512]{1,2,0:T(8,128)} %bitcast.2) | data formatting | bytes 16777216
  451.3 0.0 copy-start
  451.3 7.9 %copy.13 = f32[2,512,2048]{2,1,0:T(8,128)} copy(f32[2,512,2048]{2,1,0:T(8,128)} %get-tuple-element.20) | data formatting | bytes 16777216
  459.2 0.0 copy-done
  459.2 0.6 copy.14
Async XLA Ops:
  451.3 7.9 %copy-start = (f32[2,512]{1,0:T(2,128)S(1)}, f32[2,512]{1,0:T(2,128)}, u32[]{:S(2)}) copy-start(f32[2,512]{1,0:T(2,128)} %get-tuple-element.22) | copy-start | bytes 12292

commit v2 on v1

--- a/solution.py
+++ b/solution.py
@@ -16,8 +16,10 @@
 RING = 8
 TOK_AHEAD = 4
 TGT_SLOTS = 4
-CHUNK_F = 512
-CHUNK_B = 512
+CHUNK = 256
+DU_AHEAD = 2
+W_LAG = 2
+GAP = 1
 
 
 def dot(lhs, rhs):
@@ -36,7 +38,7 @@
 
 def kernel(n_stage, n_micro, tok_hbm, tgt_hbm, wi_hbm, wo_hbm, gain_ref,
            gwi_hbm, gwo_hbm, gg_ref, loss_ref,
-           wi, wo, agi, ago, gg, xs, dhs, of, ob, tg, da_s, u_s, sse, loss_src, loss_dst,
+           wi, wo, agi, ago, gg, xs, dhs, of, ob, tg, sse, loss_src, loss_dst,
            w_sem, out_sem, tg_sem, rx_sem, rd_sem, sf_sem, sb_sem, free_sem, lsend_sem, lrecv_sem):
     stage = lax.axis_index('stage')
     last = n_stage - 1
@@ -50,8 +52,6 @@
     for hop in range(1, n_stage):
         pl.semaphore_signal(barrier, inc=1, device_id={'stage': lax.rem(stage + hop, n_stage)},
                             device_id_type=MESH)
-    pl.semaphore_wait(barrier, n_stage - 1)
-
     def weight_copies(layer):
         return (pltpu.make_async_copy(wi_hbm.at[layer], wi.at[layer], w_sem.at[layer, 0]),
                 pltpu.make_async_copy(wo_hbm.at[layer], wo.at[layer], w_sem.at[layer, 1]))
@@ -92,9 +92,9 @@
 
     gg[...] = jnp.zeros_like(gg)
     sse[...] = jnp.zeros_like(sse)
-    for layer in range(2):
-        for copy in weight_copies(layer):
-            copy.wait()
+    for copy in weight_copies(0):
+        copy.wait()
+    pl.semaphore_wait(barrier, n_stage - 1)
 
     def gain_of(layer):
         return jnp.where(layer == 0, gain_ref[0:1, :], gain_ref[1:2, :])
@@ -102,52 +102,70 @@
     def fold(rows):
         return jnp.sum(rows.reshape(rows.shape[0] // 8, 8, rows.shape[1]), axis=0)
 
-    def forward(layer, mb):
-        x = xs[layer, mb].astype(F32)
-        inv = lax.rsqrt(jnp.mean(x * x, axis=-1, keepdims=True) + EPSILON)
-        normed = (x * inv * gain_of(layer)).astype(BF16)
-        total = x
-        for c in range(d_ff // CHUNK_F):
-            cols = pl.ds(c * CHUNK_F, CHUNK_F)
-            a = dot(normed, wi[layer, :, cols])
-            q, _ = gate(a)
-            total = total + dot((a * q).astype(BF16), wo[layer, cols, :])
-        return total.astype(BF16)
-
-    def backward(layer, mb, slot):
-        x = xs[layer, mb].astype(F32)
-        gain = gain_of(layer)
+    def normalize(x, layer):
         inv = lax.rsqrt(jnp.mean(x * x, axis=-1, keepdims=True) + EPSILON)
         xhat = x * inv
-        normed = (xhat * gain).astype(BF16)
-        dh = dhs[layer, slot]
-        dn = None
-        for c in range(d_ff // CHUNK_B):
-            cols = pl.ds(c * CHUNK_B, CHUNK_B)
-            a = dot(normed, wi[layer, :, cols])
-            du = dot_t(dh, wo[layer, cols, :])
-            q, sq = gate(a)
-            u = a * q
-            slope = q + u * (1.0 - q) * (2.0 * C0 + 6.0 * C1 * sq)
-            da = (du * slope).astype(BF16)
-            u_s[:, cols] = u.astype(BF16)
-            da_s[:, cols] = da
-            part = dot_t(da, wi[layer, :, cols])
-            dn = part if dn is None else dn + part
-        weighted = dn * gain
-        proj = jnp.mean(weighted * xhat, axis=-1, keepdims=True)
-        gg[layer] += fold(dn * xhat)
-        return (dh.astype(F32) + inv * (weighted - xhat * proj)).astype(BF16)
-
-    def weight_grads(layer, mb, slot):
-        x = xs[layer, mb].astype(F32)
-        inv = lax.rsqrt(jnp.mean(x * x, axis=-1, keepdims=True) + EPSILON)
-        normed_t = (x * inv * gain_of(layer)).astype(BF16).T
-        dh_t = dhs[layer, slot].T
-        for c in range(d_ff // CHUNK_B):
-            cols = pl.ds(c * CHUNK_B, CHUNK_B)
-            agi[layer, :, cols] += dot(normed_t, da_s[:, cols])
-            ago[layer, :, cols] += dot(dh_t, u_s[:, cols])
+        return inv, xhat, (xhat * gain_of(layer)).astype(BF16)
+
+    def compute(layer, mb_f, par_f, mb_b, slot_b, par_b):
+        chunks = d_ff // CHUNK
+        cols = [pl.ds(c * CHUNK, CHUNK) for c in range(chunks)]
+        has_f, has_b = mb_f is not None, mb_b is not None
+        du, a_b, a_f, u_b, da_b = {}, {}, {}, {}, {}
+        total = dn = None
+        if has_b:
+            dh = dhs[layer, slot_b]
+            for c in range(DU_AHEAD):
+                du[c] = dot_t(dh, wo[layer, cols[c], :])
+            x_b = xs[layer, mb_b].astype(F32)
+            inv_b, xhat_b, normed_b = normalize(x_b, layer)
+            a_b[0] = dot(normed_b, wi[layer, :, cols[0]])
+        if has_f:
+            x_f = xs[layer, mb_f].astype(F32)
+            _, _, normed_f = normalize(x_f, layer)
+            a_f[0] = dot(normed_f, wi[layer, :, cols[0]])
+        if has_b:
+            normed_t = normed_b.T
+            dh_t = dh.T
+
+        def weight_grads(c):
+            agi[layer, :, cols[c]] += dot(normed_t, da_b.pop(c))
+            ago[layer, :, cols[c]] += dot(dh_t, u_b.pop(c))
+
+        for c in range(chunks):
+            if has_b and c + DU_AHEAD < chunks:
+                du[c + DU_AHEAD] = dot_t(dh, wo[layer, cols[c + DU_AHEAD], :])
+            if c + 1 < chunks:
+                if has_b:
+                    a_b[c + 1] = dot(normed_b, wi[layer, :, cols[c + 1]])
+                if has_f:
+                    a_f[c + 1] = dot(normed_f, wi[layer, :, cols[c + 1]])
+            if has_b:
+                a = a_b.pop(c)
+                q, sq = gate(a)
+                u = a * q
+                slope = q + u * (1.0 - q) * (2.0 * C0 + 6.0 * C1 * sq)
+                da = (du.pop(c) * slope).astype(BF16)
+                u_b[c] = u.astype(BF16)
+                da_b[c] = da
+                part = dot_t(da, wi[layer, :, cols[c]])
+                dn = part if dn is None else dn + part
+            if has_f:
+                a = a_f.pop(c)
+                q, _ = gate(a)
+                part = dot((a * q).astype(BF16), wo[layer, cols[c], :])
+                total = part if total is None else total + part
+            if has_b and c >= W_LAG:
+                weight_grads(c - W_LAG)
+        if has_f:
+            of[layer, par_f] = (x_f + total).astype(BF16)
+        if has_b:
+            weighted = dn * gain_of(layer)
+            proj = jnp.mean(weighted * xhat_b, axis=-1, keepdims=True)
+            gg[layer] += fold(dn * xhat_b)
+            ob[layer, par_b] = (dh.astype(F32) + inv_b * (weighted - xhat_b * proj)).astype(BF16)
+            for c in range(chunks - W_LAG, chunks):
+                weight_grads(c)
 
     def send_f(layer, mb, target):
         par = lax.rem(mb, 2)
@@ -164,40 +182,48 @@
             send_sem=sb_sem.at[layer, par], recv_sem=rd_sem.at[layer, slot],
             device_id={'stage': target}, device_id_type=MESH)
 
-    def forward_unit(layer, mb):
+    def plan_f(layer):
         down = layer == 0
-        sends = jnp.where(down, stage < last, stage > 0)
-        receives = jnp.where(down, True, stage < last)
-        target = jnp.where(down, jnp.minimum(stage + 1, last), jnp.maximum(stage - 1, 0))
+        return (jnp.where(down, stage < last, stage > 0), jnp.where(down, True, stage < last),
+                jnp.where(down, jnp.minimum(stage + 1, last), jnp.maximum(stage - 1, 0)))
+
+    def plan_b(layer):
+        up = layer == 1
+        return (jnp.where(up, stage < last, stage > 0), jnp.where(up, stage > 0, stage < last),
+                jnp.where(up, jnp.minimum(stage + 1, last), jnp.maximum(stage - 1, 0)),
+                jnp.where(up, jnp.maximum(stage - 1, 0), jnp.minimum(stage + 1, last)))
+
+    def begin_f(layer, mb):
+        sends, receives, target = plan_f(layer)
+
+        @pl.when((layer == 0) & is_first & (mb + TOK_AHEAD < n_micro))
+        def _():
+            token_copy(mb + TOK_AHEAD).start()
+
+        @pl.when(receives)
+        def _():
+            send_f(layer, mb, target).wait_recv()
+
+        @pl.when(sends & (mb >= 2))
+        def _():
+            send_f(layer, mb - 2, target).wait_send()
+
+    def end_f(layer, mb):
+        sends, _, target = plan_f(layer)
         par = lax.rem(mb, 2)
 
-        @pl.when(down & is_first & (mb + TOK_AHEAD < n_micro))
-        def _():
-            token_copy(mb + TOK_AHEAD).start()
-
-        @pl.when(receives)
-        def _():
-            send_f(layer, mb, target).wait_recv()
-
-        @pl.when(sends & (mb >= 2))
-        def _():
-            send_f(layer, mb - 2, target).wait_send()
-
-        of[layer, par] = forward(layer, mb)
-
         @pl.when(sends)
         def _():
             send_f(layer, mb, target).start()
 
-        @pl.when(down & is_last)
+        @pl.when((layer == 0) & is_last)
         def _():
             xs[1, mb] = of[0, par]
 
-        @pl.when(jnp.logical_not(down) & is_first)
+        @pl.when((layer == 1) & is_first)
         def _():
             target_copy(mb).wait()
-            tslot = lax.rem(mb, TGT_SLOTS)
-            err = of[1, par].astype(F32) - tg[tslot].astype(F32)
+            err = of[1, par].astype(F32) - tg[lax.rem(mb, TGT_SLOTS)].astype(F32)
             dhs[1, lax.rem(mb, RING)] = (err * seed_scale).astype(BF16)
             sse[...] += fold(err * err)
 
@@ -205,14 +231,8 @@
             def _():
                 target_copy(mb + TGT_SLOTS).start()
 
-    def backward_unit(layer, mb):
-        up = layer == 1
-        sends = jnp.where(up, stage < last, stage > 0)
-        receives = jnp.where(up, stage > 0, stage < last)
-        target = jnp.where(up, jnp.minimum(stage + 1, last), jnp.maximum(stage - 1, 0))
-        source = jnp.where(up, jnp.maximum(stage - 1, 0), jnp.minimum(stage + 1, last))
-        par = lax.rem(mb, 2)
-        slot = lax.rem(mb, RING)
+    def begin_b(layer, mb):
+        sends, receives, target, _ = plan_b(layer)
 
         @pl.when(receives)
         def _():
@@ -222,21 +242,20 @@
         def _():
             send_b(layer, mb - 2, target).wait_send()
 
-        ob[layer, par] = backward(layer, mb, slot)
-
         @pl.when(sends & (mb >= RING))
         def _():
             pl.semaphore_wait(free_sem.at[layer], 1)
 
+    def end_b(layer, mb):
+        sends, receives, target, source = plan_b(layer)
+
         @pl.when(sends)
         def _():
             send_b(layer, mb, target).start()
 
-        @pl.when(up & is_last)
-        def _():
-            dhs[0, slot] = ob[1, par]
-
-        weight_grads(layer, mb, slot)
+        @pl.when((layer == 1) & is_last)
+        def _():
+            dhs[0, lax.rem(mb, RING)] = ob[1, lax.rem(mb, 2)]
 
         @pl.when(receives & (mb + RING < n_micro))
         def _():
@@ -252,33 +271,57 @@
             src_ref=loss_src, dst_ref=loss_dst, send_sem=lsend_sem.at[peer - 1], recv_sem=lrecv_sem.at[0],
             device_id={'stage': peer}, device_id_type=MESH)
 
-    ticks = n_micro + 4 * last
-
-    @pl.loop(0, ticks)
-    def _(tick):
-        @pl.loop(0, 2)
-        def _(layer):
-            mb = tick - jnp.where(layer == 0, stage, 2 * last - stage)
-
-            @pl.when((mb >= 0) & (mb < n_micro))
-            def _():
-                forward_unit(layer, mb)
-
-        @pl.when(is_first & (tick == n_micro - 1 + 2 * last))
+    gap = GAP if n_stage > 2 else 0
+    pos, end = stage + jnp.where(stage >= n_stage // 2, gap, 0), last + gap
+    ticks = n_micro + 4 * end + 2
+
+    @pl.loop(0, 2 * ticks)
+    def _(step):
+        tick, layer = step // 2, lax.rem(step, 2)
+        mb_f = tick - jnp.where(layer == 0, pos, 2 * end - pos)
+        mb_b = tick - jnp.where(layer == 1, 2 * end + 1 + pos, 4 * end + 2 - pos)
+        ok_f = (mb_f >= 0) & (mb_f < n_micro)
+        ok_b = (mb_b >= 0) & (mb_b < n_micro)
+
+        @pl.when(step == 1)
+        def _():
+            for copy in weight_copies(1):
+                copy.wait()
+
+        @pl.when(ok_f)
+        def _():
+            begin_f(layer, mb_f)
+
+        @pl.when(ok_b)
+        def _():
+            begin_b(layer, mb_b)
+
+        @pl.when(ok_f & ok_b)
+        def _():
+            compute(layer, mb_f, lax.rem(mb_f, 2), mb_b, lax.rem(mb_b, RING), lax.rem(mb_b, 2))
+
+        @pl.when(ok_f & jnp.logical_not(ok_b))
+        def _():
+            compute(layer, mb_f, lax.rem(mb_f, 2), None, None, None)
+
+        @pl.when(ok_b & jnp.logical_not(ok_f))
+        def _():
+            compute(layer, None, None, mb_b, lax.rem(mb_b, RING), lax.rem(mb_b, 2))
+
+        @pl.when(ok_f)
+        def _():
+            end_f(layer, mb_f)
+
+        @pl.when(ok_b)
+        def _():
+            end_b(layer, mb_b)
+
+        @pl.when(is_first & (layer == 1) & (mb_f == n_micro - 1))
         def _():
             total = jnp.sum(sse[...]) / (n_micro * tokens_mb * d_model)
             loss_src[...] = jnp.full(loss_src.shape, total, F32)
             for peer in range(1, n_stage):
                 loss_copy(peer).start()
-
-        @pl.loop(0, 2)
-        def _(index):
-            layer = 1 - index
-            mb = tick - jnp.where(layer == 1, 2 * last + stage, 4 * last - stage)
-
-            @pl.when((mb >= 0) & (mb < n_micro))
-            def _():
-                backward_unit(layer, mb)
 
     gg_ref[...] = jnp.sum(gg[...], axis=1)
 
@@ -341,8 +384,6 @@
                 pltpu.VMEM((2, 2, tokens_mb, d_model), BF16),
                 pltpu.VMEM((2, 2, tokens_mb, d_model), BF16),
                 pltpu.VMEM((TGT_SLOTS, tokens_mb, d_model), BF16),
-                pltpu.VMEM((tokens_mb, d_ff), BF16),
-                pltpu.VMEM((tokens_mb, d_ff), BF16),
                 pltpu.VMEM((8, d_model), F32),
                 pltpu.VMEM((8, 128), F32),
                 pltpu.VMEM((8, 128), F32),

time: 462 us -> 374 us (0.81)
  Pallas kernels: 442 us -> 354 us
    pallas_call x1, Pallas kernels: 442 us -> 354 us  [device_step(): pl.pallas_call(functools.partial(kernel, n_stage, n_micro), out_shape=(ja...]
where the time goes in v2:
time: 374 us; the launch traced here: 373 us
  Pallas kernels  354 us (95%)
  local copies, waits for them, and re-layouts  17.2 us (5%)
    pallas_call x1, Pallas kernels, device_step(): pl.pallas_call(functools.partial(kernel, n_stage, n_micro), out_shape=(ja...  354 us
    unnamed x5, local copies, waits for them, and re-layouts  17.2 us

profile of v2, /device:TPU:0, one launch (start us, length us, event | category | flops | bytes accessed | tf_op | source)
XLA Modules:
  0.0 373.4 jit_solution(6244162727211310231)
XLA Ops:
  0.6 353.8 %shard_map.84 = (f32[2,512,2048]{2,1,0:T(8,128)}, f32[2,512,2048]{2,1,0:T(8,128)}, f32[2,512]{1,0:T(2,128)}, f32[1,1]{1,0:T(1,128)}) custom-call(bf16[32,256,512]{2,1,0:T(8,128)(2,1)} %tok_hbm.1, bf16[32,256,512]{2,1,0:T(8,128)(2,1)} %tgt_hbm.1, bf16[2,512,2048]{2,1,0:T(8,128)(2,1)} %wi_hbm.1, bf16[2,2048,512]{2,1,0:T(8,128)(2,1)} %wo_hbm.1, f32[2,512]{1,0:T(2,128)} %gain_ref.1), custom_call_target="tpu_custom_call" | custom-call | tf_op jit(solution)/shard_map/pallas_call | solution.py:367
  354.4 8.7 %copy.9 = f32[2,2048,512]{2,1,0:T(8,128)} copy(f32[2,2048,512]{1,2,0:T(8,128)} %bitcast.2) | data formatting | bytes 16777216
  363.1 0.0 copy-start
  363.1 7.9 %copy.13 = f32[2,512,2048]{2,1,0:T(8,128)} copy(f32[2,512,2048]{2,1,0:T(8,128)} %get-tuple-element.20) | data formatting | bytes 16777216
  371.0 0.0 copy-done
  371.0 0.6 copy.14
Async XLA Ops:
  363.1 7.9 %copy-start = (f32[2,512]{1,0:T(2,128)S(1)}, f32[2,512]{1,0:T(2,128)}, u32[]{:S(2)}) copy-start(f32[2,512]{1,0:T(2,128)} %get-tuple-element.22) | copy-start | bytes 12292

commit v3 on v2

--- a/solution.py
+++ b/solution.py
@@ -13,13 +13,15 @@
 BF16 = jnp.bfloat16
 C0 = 0.7978845608028654
 C1 = C0 * 0.044715
-RING = 8
+RING = 4
 TOK_AHEAD = 4
-TGT_SLOTS = 4
+TGT_SLOTS = 2
 CHUNK = 256
 DU_AHEAD = 2
+A_AHEAD = 1
 W_LAG = 2
 GAP = 1
+VMEM_LIMIT = 67043328 - 16 * 2**20
 
 
 def dot(lhs, rhs):
@@ -37,9 +39,9 @@
 
 
 def kernel(n_stage, n_micro, tok_hbm, tgt_hbm, wi_hbm, wo_hbm, gain_ref,
-           gwi_hbm, gwo_hbm, gg_ref, loss_ref,
-           wi, wo, agi, ago, gg, xs, dhs, of, ob, tg, sse, loss_src, loss_dst,
-           w_sem, out_sem, tg_sem, rx_sem, rd_sem, sf_sem, sb_sem, free_sem, lsend_sem, lrecv_sem):
+           agi, ago, gg_ref, loss_ref, slope_hbm, hid_hbm,
+           wi, wo, gg, xs, dhs, of, ob, tg, slope_out, hid_out, slope_in, hid_in, sse, loss_src, loss_dst,
+           w_sem, tg_sem, rx_sem, rd_sem, sf_sem, sb_sem, free_sem, lsend_sem, lrecv_sem, keep_sem, fetch_sem):
     stage = lax.axis_index('stage')
     last = n_stage - 1
     is_first = stage == 0
@@ -63,10 +65,6 @@
         slot = lax.rem(mb, TGT_SLOTS)
         return pltpu.make_async_copy(tgt_hbm.at[mb], tg.at[slot], tg_sem.at[slot])
 
-    def out_copies(layer):
-        return (pltpu.make_async_copy(agi.at[layer], gwi_hbm.at[layer], out_sem.at[layer, 0]),
-                pltpu.make_async_copy(ago.at[layer], gwo_hbm.at[layer], out_sem.at[layer, 1]))
-
     for copy in weight_copies(0):
         copy.start()
 
@@ -88,7 +86,11 @@
         layer, row = i // (d_model // 8), lax.rem(i, d_model // 8)
         rows = pl.ds(pl.multiple_of(row * 8, 8), 8)
         agi[layer, rows, :] = jnp.zeros((8, d_ff), F32)
-        ago[layer, rows, :] = jnp.zeros((8, d_ff), F32)
+
+    @pl.loop(0, 2 * d_ff // 32)
+    def _(i):
+        layer, row = i // (d_ff // 32), lax.rem(i, d_ff // 32)
+        ago[layer, pl.ds(pl.multiple_of(row * 32, 32), 32), :] = jnp.zeros((32, d_model), F32)
 
     gg[...] = jnp.zeros_like(gg)
     sse[...] = jnp.zeros_like(sse)
@@ -111,49 +113,44 @@
         chunks = d_ff // CHUNK
         cols = [pl.ds(c * CHUNK, CHUNK) for c in range(chunks)]
         has_f, has_b = mb_f is not None, mb_b is not None
-        du, a_b, a_f, u_b, da_b = {}, {}, {}, {}, {}
+        du, a_f, da_b = {}, {}, {}
         total = dn = None
         if has_b:
             dh = dhs[layer, slot_b]
             for c in range(DU_AHEAD):
                 du[c] = dot_t(dh, wo[layer, cols[c], :])
-            x_b = xs[layer, mb_b].astype(F32)
-            inv_b, xhat_b, normed_b = normalize(x_b, layer)
-            a_b[0] = dot(normed_b, wi[layer, :, cols[0]])
         if has_f:
             x_f = xs[layer, mb_f].astype(F32)
             _, _, normed_f = normalize(x_f, layer)
-            a_f[0] = dot(normed_f, wi[layer, :, cols[0]])
+            for c in range(A_AHEAD):
+                a_f[c] = dot(normed_f, wi[layer, :, cols[c]])
         if has_b:
+            x_b = xs[layer, mb_b].astype(F32)
+            inv_b, xhat_b, normed_b = normalize(x_b, layer)
             normed_t = normed_b.T
-            dh_t = dh.T
 
         def weight_grads(c):
             agi[layer, :, cols[c]] += dot(normed_t, da_b.pop(c))
-            ago[layer, :, cols[c]] += dot(dh_t, u_b.pop(c))
+            ago[layer, cols[c], :] += dot(hid_in[layer, :, cols[c]].T, dh)
 
         for c in range(chunks):
             if has_b and c + DU_AHEAD < chunks:
                 du[c + DU_AHEAD] = dot_t(dh, wo[layer, cols[c + DU_AHEAD], :])
-            if c + 1 < chunks:
-                if has_b:
-                    a_b[c + 1] = dot(normed_b, wi[layer, :, cols[c + 1]])
-                if has_f:
-                    a_f[c + 1] = dot(normed_f, wi[layer, :, cols[c + 1]])
+            if has_f and c + A_AHEAD < chunks:
+                a_f[c + A_AHEAD] = dot(normed_f, wi[layer, :, cols[c + A_AHEAD]])
             if has_b:
-                a = a_b.pop(c)
-                q, sq = gate(a)
-                u = a * q
-                slope = q + u * (1.0 - q) * (2.0 * C0 + 6.0 * C1 * sq)
-                da = (du.pop(c) * slope).astype(BF16)
-                u_b[c] = u.astype(BF16)
+                da = (du.pop(c) * slope_in[layer, :, cols[c]]).astype(BF16)
                 da_b[c] = da
                 part = dot_t(da, wi[layer, :, cols[c]])
                 dn = part if dn is None else dn + part
             if has_f:
                 a = a_f.pop(c)
-                q, _ = gate(a)
-                part = dot((a * q).astype(BF16), wo[layer, cols[c], :])
+                q, sq = gate(a)
+                u = a * q
+                slope_out[layer, :, cols[c]] = q + u * (1.0 - q) * (2.0 * C0 + 6.0 * C1 * sq)
+                hid = u.astype(BF16)
+                hid_out[layer, :, cols[c]] = hid
+                part = dot(hid, wo[layer, cols[c], :])
                 total = part if total is None else total + part
             if has_b and c >= W_LAG:
                 weight_grads(c - W_LAG)
@@ -167,6 +164,14 @@
             for c in range(chunks - W_LAG, chunks):
                 weight_grads(c)
 
+    def keep_copies(layer, mb):
+        return (pltpu.make_async_copy(slope_out.at[layer], slope_hbm.at[layer, mb], keep_sem.at[layer, 0]),
+                pltpu.make_async_copy(hid_out.at[layer], hid_hbm.at[layer, mb], keep_sem.at[layer, 1]))
+
+    def fetch_copies(layer, mb):
+        return (pltpu.make_async_copy(slope_hbm.at[layer, mb], slope_in.at[layer], fetch_sem.at[layer, 0]),
+                pltpu.make_async_copy(hid_hbm.at[layer, mb], hid_in.at[layer], fetch_sem.at[layer, 1]))
+
     def send_f(layer, mb, target):
         par = lax.rem(mb, 2)
         return pltpu.make_async_remote_copy(
@@ -261,11 +266,6 @@
         def _():
             pl.semaphore_signal(free_sem.at[layer], inc=1, device_id={'stage': source}, device_id_type=MESH)
 
-        @pl.when(mb == n_micro - 1)
-        def _():
-            for copy in out_copies(layer):
-                copy.start()
-
     def loss_copy(peer):
         return pltpu.make_async_remote_copy(
             src_ref=loss_src, dst_ref=loss_dst, send_sem=lsend_sem.at[peer - 1], recv_sem=lrecv_sem.at[0],
@@ -273,21 +273,39 @@
 
     gap = GAP if n_stage > 2 else 0
     pos, end = stage + jnp.where(stage >= n_stage // 2, gap, 0), last + gap
-    ticks = n_micro + 4 * end + 2
+    ticks = n_micro + 4 * end + 3
+
+    def index_f(tick, layer):
+        return tick - jnp.where(layer == 0, pos, 2 * end - pos)
+
+    def index_b(tick, layer):
+        return tick - jnp.where(layer == 1, 2 * end + 2 + pos, 4 * end + 3 - pos)
+
+    def inside(mb):
+        return (mb >= 0) & (mb < n_micro)
 
     @pl.loop(0, 2 * ticks)
     def _(step):
         tick, layer = step // 2, lax.rem(step, 2)
-        mb_f = tick - jnp.where(layer == 0, pos, 2 * end - pos)
-        mb_b = tick - jnp.where(layer == 1, 2 * end + 1 + pos, 4 * end + 2 - pos)
-        ok_f = (mb_f >= 0) & (mb_f < n_micro)
-        ok_b = (mb_b >= 0) & (mb_b < n_micro)
+        mb_f, mb_b = index_f(tick, layer), index_b(tick, layer)
+        ok_f, ok_b = inside(mb_f), inside(mb_b)
+        next_b = index_b((step + 1) // 2, 1 - layer)
 
         @pl.when(step == 1)
         def _():
             for copy in weight_copies(1):
                 copy.wait()
 
+        @pl.when(inside(mb_f - 1))
+        def _():
+            for copy in keep_copies(layer, mb_f - 1):
+                copy.wait()
+
+        @pl.when(inside(next_b))
+        def _():
+            for copy in fetch_copies(1 - layer, next_b):
+                copy.start()
+
         @pl.when(ok_f)
         def _():
             begin_f(layer, mb_f)
@@ -295,6 +313,8 @@
         @pl.when(ok_b)
         def _():
             begin_b(layer, mb_b)
+            for copy in fetch_copies(layer, mb_b):
+                copy.wait()
 
         @pl.when(ok_f & ok_b)
         def _():
@@ -315,6 +335,11 @@
         @pl.when(ok_b)
         def _():
             end_b(layer, mb_b)
+
+        @pl.when(ok_f)
+        def _():
+            for copy in keep_copies(layer, mb_f):
+                copy.start()
 
         @pl.when(is_first & (layer == 1) & (mb_f == n_micro - 1))
         def _():
@@ -352,9 +377,6 @@
             for mb in (n_micro - 2, n_micro - 1):
                 send_b(layer, mb, b_target).wait_send()
 
-        for copy in out_copies(layer):
-            copy.wait()
-
 
 def solution(mesh):
     n_stage = mesh.shape['stage']
@@ -364,37 +386,41 @@
         d_ff = w_in.shape[2]
         any_spec = pl.BlockSpec(memory_space=pl.ANY)
         dma = pltpu.SemaphoreType.DMA
-        grad_w_in, grad_w_out_t, grad_gains, loss = pl.pallas_call(
+        grad_w_in, grad_w_out, grad_gains, loss, _, _ = pl.pallas_call(
             functools.partial(kernel, n_stage, n_micro),
-            out_shape=(jax.ShapeDtypeStruct((2, d_model, d_ff), F32),
-                       jax.ShapeDtypeStruct((2, d_model, d_ff), F32),
+            out_shape=(pltpu.VMEM((2, d_model, d_ff), F32),
+                       pltpu.VMEM((2, d_ff, d_model), F32),
                        jax.ShapeDtypeStruct((2, d_model), F32),
-                       jax.ShapeDtypeStruct((1, 1), F32)),
+                       jax.ShapeDtypeStruct((1, 1), F32),
+                       jax.ShapeDtypeStruct((2, n_micro, tokens_mb, d_ff), F32),
+                       jax.ShapeDtypeStruct((2, n_micro, tokens_mb, d_ff), BF16)),
             in_specs=[any_spec] * 4 + [pl.BlockSpec(memory_space=pltpu.VMEM)],
-            out_specs=(any_spec, any_spec, pl.BlockSpec(memory_space=pltpu.VMEM),
-                       pl.BlockSpec(memory_space=pltpu.SMEM)),
+            out_specs=(pl.BlockSpec(memory_space=pltpu.VMEM),) * 3 + (
+                       pl.BlockSpec(memory_space=pltpu.SMEM), any_spec, any_spec),
             scratch_shapes=[
                 pltpu.VMEM((2, d_model, d_ff), BF16),
                 pltpu.VMEM((2, d_ff, d_model), BF16),
-                pltpu.VMEM((2, d_model, d_ff), F32),
-                pltpu.VMEM((2, d_model, d_ff), F32),
                 pltpu.VMEM((2, 8, d_model), F32),
                 pltpu.VMEM((2, n_micro, tokens_mb, d_model), BF16),
                 pltpu.VMEM((2, RING, tokens_mb, d_model), BF16),
                 pltpu.VMEM((2, 2, tokens_mb, d_model), BF16),
                 pltpu.VMEM((2, 2, tokens_mb, d_model), BF16),
                 pltpu.VMEM((TGT_SLOTS, tokens_mb, d_model), BF16),
+                pltpu.VMEM((2, tokens_mb, d_ff), F32),
+                pltpu.VMEM((2, tokens_mb, d_ff), BF16),
+                pltpu.VMEM((2, tokens_mb, d_ff), F32),
+                pltpu.VMEM((2, tokens_mb, d_ff), BF16),
                 pltpu.VMEM((8, d_model), F32),
                 pltpu.VMEM((8, 128), F32),
                 pltpu.VMEM((8, 128), F32),
-                dma((2, 2)), dma((2, 2)), dma((TGT_SLOTS,)), dma((2, n_micro)), dma((2, RING)),
+                dma((2, 2)), dma((TGT_SLOTS,)), dma((2, n_micro)), dma((2, RING)),
                 dma((2, 2)), dma((2, 2)), pltpu.SemaphoreType.REGULAR((2,)),
-                dma((n_stage - 1,)), dma((1,)),
+                dma((n_stage - 1,)), dma((1,)), dma((2, 2)), dma((2, 2)),
             ],
             compiler_params=pltpu.CompilerParams(
-                collective_id=0, has_side_effects=True, vmem_limit_bytes=67043328),
+                collective_id=0, has_side_effects=True, vmem_limit_bytes=VMEM_LIMIT),
         )(tokens, targets, w_in, w_out, norm_gains)
-        return grad_w_in, jnp.swapaxes(grad_w_out_t, 1, 2), grad_gains, loss.reshape(1)
+        return grad_w_in, grad_w_out, grad_gains, loss.reshape(1)
 
     block_spec = P(('dp', 'stage'))
     return jax.shard_map(device_step, mesh=mesh,

time: 374 us -> 335 us (0.90)
  Pallas kernels: 354 us -> 325 us
  local copies, waits for them, and re-layouts: 17.2 us -> 7.39 us
    pallas_call x1, Pallas kernels: 354 us -> 325 us  [device_step(): pl.pallas_call(functools.partial(kernel, n_stage, n_micro), out_shape=(pl...]
    unnamed x5, local copies, waits for them, and re-layouts: 17.2 us -> 7.39 us
where the time goes in v3:
time: 335 us; the launch traced here: 334 us
  Pallas kernels  325 us (97%)
  local copies, waits for them, and re-layouts  7.39 us (2%)
    pallas_call x1, Pallas kernels, device_step(): pl.pallas_call(functools.partial(kernel, n_stage, n_micro), out_shape=(pl...  325 us
    unnamed x5, local copies, waits for them, and re-layouts  7.39 us

profile of v3, /device:TPU:0, one launch (start us, length us, event | category | flops | bytes accessed | tf_op | source)
XLA Modules:
  0.0 334.4 jit_solution(3248879141841033932)
XLA Ops:
  0.6 324.6 %shard_map.84 = (f32[2,512,2048]{2,1,0:T(8,128)S(1)}, f32[2,2048,512]{2,1,0:T(8,128)S(1)}, f32[2,512]{1,0:T(2,128)}, f32[1,1]{1,0:T(1,128)}, f32[2,32,256,2048]{...) custom-call(bf16[32,256,512]{2,1,0:T(8,128)(2,1)} %tok_hbm.1, bf16[32,256,512]{2,1,0:T(8,128)(2,1)} %tgt_hbm.1, ...), custom_call_target="tpu_custom_call" | custom-call | tf_op jit(solution)/shard_map/pallas_call | solution.py:389
  325.2 3.4 %copy.13 = f32[2,512,2048]{2,1,0:T(8,128)} copy(f32[2,512,2048]{2,1,0:T(8,128)S(1)} %get-tuple-element.12) | data formatting | bytes 16777216
  328.6 0.0 copy-start
  328.6 3.4 %copy.14 = f32[2,2048,512]{2,1,0:T(8,128)} copy(f32[2,2048,512]{2,1,0:T(8,128)S(1)} %get-tuple-element.13) | data formatting | bytes 16777216
  332.0 0.0 copy-done
  332.0 0.6 copy.15
Async XLA Ops:
  328.6 3.4 %copy-start = (f32[2,512]{1,0:T(2,128)S(1)}, f32[2,512]{1,0:T(2,128)}, u32[]{:S(2)}) copy-start(f32[2,512]{1,0:T(2,128)} %get-tuple-element.22) | copy-start | bytes 12292
